TPU v7x, 32 devices: a whole 2x2x4 slice. The times are simulated.
32 devices in a mesh: seq: 32 (over z, y, x, core), head: 1.
Axes of the slice: x: 2, y: 2, z: 4, core: 2. Of those that a mesh axis runs over, the one named last changes fastest.
Arguments:
- hidden: bfloat16 [4096, 1024], P('seq'), may hold values from -6 to 6
- query_weight: bfloat16 [1024, 512], P(None, 'head'), may hold values from -0.1875 to 0.1875
- key_weight: bfloat16 [1024, 512], P(None, 'head'), may hold values from -0.1875 to 0.1875
- values: bfloat16 [4096, 512], P('seq', 'head'), may hold values from -6 to 6
- grad_out: bfloat16 [4096, 512], P('seq', 'head'), may hold values from -6 to 6
- random_feats: float32 [8, 64, 256], P('head'), may hold values from -4 to 4
Outputs:
- grad_hidden: float32 [4096, 1024], P('seq')
- grad_values: bfloat16 [4096, 512], P('seq', 'head')
- grad_query_weight: float32 [1024, 512], P('seq', 'head')
- grad_key_weight: float32 [1024, 512], P('seq', 'head')
All inputs are finite; a program needn't handle non-finite values.
Results may differ from a plain program's by a relative error of at most 0.0038.
Values sent between devices are 32-bit elements; how exact they have to be, the bound alone decides.
A program may use at most 64 MiB of HBM per device.

v0:
```python
import jax
import jax.numpy as jnp
from jax import lax
from jax.sharding import PartitionSpec as P

HIGH = lax.Precision.HIGHEST


def features(rows, table, feat_count):
    logits = jnp.einsum("tgd,gdm->gtm", rows, table, precision=HIGH)
    half_norm = 0.5 * jnp.sum(rows * rows, axis=2).T
    return jnp.exp(logits - half_norm[:, :, None]) * feat_count ** (-0.5)


def feature_grad(rows, feats, grads, table, feature_scale, tok_count):
    weighted = feats * grads
    back = jnp.einsum("gtm,gdm->tgd", weighted, table, precision=HIGH)
    totals = jnp.sum(weighted, axis=2).T
    result = (back - rows * totals[:, :, None]) * feature_scale
    return result.reshape(tok_count, -1).astype(jnp.bfloat16)


def back_product(grads, weight):
    return lax.dot_general(
        grads, weight, (((1,), (1,)), ((), ())), preferred_element_type=jnp.float32
    )


def shards(hidden, query_weight, key_weight, values, grad_out, random_feats):
    tok_count = hidden.shape[0]
    group_count = random_feats.shape[0]
    head_dim = random_feats.shape[1]
    feat_count = random_feats.shape[2]
    feature_scale = head_dim ** (-0.25)
    query_proj = jnp.dot(hidden, query_weight, preferred_element_type=jnp.float32)
    key_proj = jnp.dot(hidden, key_weight, preferred_element_type=jnp.float32)
    query_rows = (query_proj * feature_scale).reshape(tok_count, group_count, head_dim)
    key_rows = (key_proj * feature_scale).reshape(tok_count, group_count, head_dim)
    value_rows = values.astype(jnp.float32).reshape(tok_count, group_count, head_dim)
    key_feats = features(key_rows, random_feats, feat_count)
    local_state = jnp.einsum("tgj,gtm->gjm", value_rows, key_feats, precision=HIGH)
    local_normal = jnp.sum(key_feats, axis=1)
    value_state, normalizer = lax.psum((local_state, local_normal), "seq")
    query_feats = features(query_rows, random_feats, feat_count)
    numerator = jnp.einsum("gtm,gjm->tgj", query_feats, value_state, precision=HIGH)
    denominator = jnp.einsum("gtm,gm->tg", query_feats, normalizer, precision=HIGH)
    attended = numerator / denominator[:, :, None]
    upstream = grad_out.astype(jnp.float32).reshape(tok_count, group_count, head_dim)
    grad_numer = upstream / denominator[:, :, None]
    grad_denom = -jnp.sum(upstream * attended, axis=2) / denominator
    grad_qfeat = (
        jnp.einsum("tgj,gjm->gtm", grad_numer, value_state, precision=HIGH)
        + grad_denom.T[:, :, None] * normalizer[:, None, :]
    )
    part_state = jnp.einsum("gtm,tgj->gjm", query_feats, grad_numer, precision=HIGH)
    part_normal = jnp.einsum("gtm,tg->gm", query_feats, grad_denom, precision=HIGH)
    grad_query = feature_grad(
        query_rows, query_feats, grad_qfeat, random_feats, feature_scale, tok_count
    )
    grad_state, grad_normal = lax.psum((part_state, part_normal), "seq")
    grad_kfeat = (
        jnp.einsum("tgj,gjm->gtm", value_rows, grad_state, precision=HIGH) + grad_normal[:, None, :]
    )
    grad_value = jnp.einsum("gtm,gjm->tgj", key_feats, grad_state, precision=HIGH)
    grad_values = grad_value.reshape(tok_count, -1).astype(jnp.bfloat16)
    grad_key = feature_grad(key_rows, key_feats, grad_kfeat, random_feats, feature_scale, tok_count)
    both_parts = back_product(grad_query, query_weight) + back_product(grad_key, key_weight)
    grad_hidden = lax.psum(both_parts, "head")
    col_count = grad_query.shape[1]
    combined = jnp.concatenate((grad_query, grad_key), axis=1)
    stacked = lax.psum_scatter(
        lax.dot_general(
            hidden, combined, (((0,), (0,)), ((), ())), preferred_element_type=jnp.float32
        ),
        "seq",
        scatter_dimension=0,
        tiled=True,
    )
    grad_query_weight = stacked[:, :col_count]
    grad_key_weight = stacked[:, col_count:]
    return (grad_hidden, grad_values, grad_query_weight, grad_key_weight)


def solution(mesh):
    placed = (
        P("seq", None),
        P(None, "head"),
        P(None, "head"),
        P("seq", "head"),
        P("seq", "head"),
        P("head", None, None),
    )
    return jax.shard_map(
        shards,
        mesh=mesh,
        in_specs=placed,
        out_specs=(P("seq", None), P("seq", "head"), P("seq", "head"), P("seq", "head")),
        check_vma=False,
    )
```

profile of v0, /device:TPU:0, one launch (start us, length us, event | category | flops | bytes accessed | tf_op | source)
XLA Modules:
  0.0 406.6 jit_solution(10344959383885730402)
XLA Ops:
  7.2 1.1 copy.32
  8.4 1.7 copy.30
  10.1 1.3 convolution_multiply_fusion.1
  11.6 1.7 convolution_multiply_fusion
  13.4 1.2 fusion.24
  14.6 42.1 %psum.31 = f32[8,256]{1,0:T(8,128)S(1)} all-reduce(f32[8,256]{1,0:T(8,128)S(1)} %get-tuple-element.20), channel_id=1, replica_groups=mesh['seq'=32,'head'=1] {'seq'}, use_global_device_ids=true, to_apply=%region_3.0 | all-reduce | flops 2048 | bytes 16384 | tf_op jit(solution)/shard_map/psum | solution.py:43
  56.7 2.3 fusion.6
  59.0 1.0 fusion.20
  59.9 2.5 fusion.19
  62.4 1.3 convolution_bitcast_fusion.1
  63.8 131.0 %all-reduce.3.cloned.1.call-done = (f32[8,64,256]{2,1,0:T(8,128)}, f32[8,64,256]{2,1,0:T(8,128)}) async-done(((f32[8,64,256]{2,1,0:T(8,128)}, f32[8,64,256]{2,1,0:T(8,128)}), (f32[8,64,256]{2,1,0:T(8,128)}, f32[8,64,256]{2,1,0:T(8,128)})) %all-reduce.3.cloned.1.call-update) | async-done | bytes 1048592 | tf_op jit(solution)/shard_map/psum | solution.py:43
  194.8 2.3 fusion.15
  197.8 3.2 fusion.25
  201.0 39.4 %psum.34 = f32[8,256]{1,0:T(8,128)S(1)} all-reduce(f32[8,256]{1,0:T(8,128)S(1)} %bitcast.113), channel_id=1, replica_groups=mesh['seq'=32,'head'=1] {'seq'}, use_global_device_ids=true, to_apply=%region_8.0 | all-reduce | flops 2048 | bytes 16384 | tf_op jit(solution)/shard_map/psum | solution.py:60
  240.4 2.7 fusion.13
  243.1 1.8 fusion.26
  244.9 2.3 fusion.14
  247.3 2.7 convolution_bitcast_fusion
  249.9 5.3 %copy.42 = f32[1024,1024]{1,0:T(8,128)} copy(f32[1024,1024]{0,1:T(8,128)} %convolution_bitcast_fusion) | data formatting | bytes 8388608
  255.3 2.3 convolution_convert_fusion
  257.6 0.8 copy.34
  258.9 1.3 convolution_add_fusion.2
  260.2 138.0 %reduce-scatter.4.cloned.1.call-done = f32[32,1024]{1,0:T(8,128)} async-done(((f32[1024,1024]{1,0:T(8,128)}), f32[32,1024]{1,0:T(8,128)}) %reduce-scatter.4.cloned.1.call-update) | async-done | bytes 131088
  398.2 1.5 fusion.23
  (29 shorter events, 1.6 us)
Async XLA Ops:
  7.2 2.9 copy-start
  7.2 6.2 %copy-start.1 = (f32[8,64,256]{2,1,0:T(8,128)S(1)}, f32[8,64,256]{2,1,0:T(8,128)}, u32[]{:S(2)}) copy-start(f32[8,64,256]{2,1,0:T(8,128)} %param.11) | copy-start | bytes 1572868
  7.2 187.6 %all-reduce.3.cloned.1.call-start = ((), (), s32[]{:S(2)}) async-start(), calls=%async_computation.2 | async-start | bytes 2097152 | tf_op jit(solution)/shard_map/psum | solution.py:43
  11.5 45.2 %copy-start.2 = (f32[128,512]{0,1:T(8,128)}, f32[128,512]{0,1:T(8,128)S(1)}, u32[]{:S(2)}) copy-start(f32[128,512]{0,1:T(8,128)S(1)} %copy.29) | copy-start | bytes 786436
  63.7 334.5 %reduce-scatter.4.cloned.1.call-start = ((), (), s32[]{:S(2)}) async-start(), calls=%async_computation.1 | async-start | bytes 4325376
  201.0 46.2 %copy-start.4 = (bf16[128,1024]{1,0:T(8,128)(2,1)S(1)}, bf16[128,1024]{1,0:T(8,128)(2,1)}, u32[]{:S(2)}) copy-start(bf16[128,1024]{1,0:T(8,128)(2,1)} %param.6) | copy-start | bytes 786436
  243.1 6.8 %copy-start.5 = (bf16[128,8,64]{0,2,1:T(8,128)(2,1)}, bf16[128,8,64]{0,2,1:T(8,128)(2,1)S(1)}, u32[]{:S(2)}) copy-start(bf16[128,8,64]{0,2,1:T(8,128)(2,1)S(1)} %fusion.13) | copy-start | bytes 393220
  255.3 3.1 copy-start.6
  255.3 3.6 copy-start.3
Sparse Core Ops, SparseCore 0:
  63.8 130.9 all-reduce.2
  255.4 142.7 reduce-scatter.3
where the time goes:
time: 407 us
  waiting for transfers between devices  269 us (66%)
  blocking collectives  81.4 us (20%)
  matrix products  30.9 us (8%)
  between operations  14.2 us (3%)
  local copies, waits for them, and re-layouts  10.8 us (3%)
    unnamed x3, waiting for transfers between devices  138 us
    psum x1, waiting for transfers between devices, shards(): value_state, normalizer = lax.psum((local_state, local_normal), 'seq')  131 us
    psum x1, blocking collectives, shards(): value_state, normalizer = lax.psum((local_state, local_normal), 'seq')  42.1 us
    psum x1, blocking collectives, shards(): grad_state, grad_normal = lax.psum((part_state, part_normal), 'seq')  39.4 us
  transfers between devices with their start and end apart: 2, of which 2 were waited for; matrix products, arithmetic and copies ran while one was open for 1% of the time, Pallas kernels for 0%

commit v1 on v0

v1 whole, which is shorter than its diff:
```python
import functools

import jax
import jax.numpy as jnp
from jax import lax
from jax.experimental import pallas as pl
from jax.experimental.pallas import tpu as pltpu
from jax.sharding import PartitionSpec as P

HIGHEST = lax.Precision.HIGHEST
HIGH = lax.Precision.HIGH
LANES = 128


def phase_orders(count):
    depth = count.bit_length() - 1
    middle = list(range(1, depth - 1))
    return [[0] + middle[s:] + middle[:s] + [depth - 1] for s in range(3)]


class Peers:
    def __init__(self, count):
        self.count = count
        self.depth = count.bit_length() - 1
        self.me = lax.axis_index("seq")
        self.bits = [(self.me // 2**b) % 2 for b in range(self.depth)]
        self.ids = [self.me + (1 - 2 * self.bits[b]) * 2**b for b in range(self.depth)]

    def greet(self):
        barrier = pltpu.get_barrier_semaphore()
        for peer in self.ids:
            pl.semaphore_signal(
                barrier, inc=1, device_id={"seq": peer}, device_id_type=pl.DeviceIdType.MESH
            )
        pl.semaphore_wait(barrier, self.depth)

    def send(self, src, dst, sends, recvs, bit):
        copy = pltpu.make_async_remote_copy(
            src_ref=src,
            dst_ref=dst,
            send_sem=sends,
            recv_sem=recvs,
            device_id={"seq": self.ids[bit]},
            device_id_type=pl.DeviceIdType.MESH,
        )
        copy.start()
        return copy


class Halving:
    def __init__(self, peers, order, buf, recv, sends, recvs):
        self.peers, self.order = peers, order
        self.buf, self.recv, self.sends, self.recvs = buf, recv, sends, recvs
        self.offs = [0]
        for p, bit in enumerate(order):
            self.offs.append(self.offs[-1] + peers.bits[bit] * (peers.count >> (p + 1)))
        self.place = self.offs[-1]

    def start(self, p):
        half = self.peers.count >> (p + 1)
        bit = self.order[p]
        other = self.offs[p] + (1 - self.peers.bits[bit]) * half
        self.landed = self.recv.at[pl.ds(self.peers.count - 2 * half, half)]
        self.copy = self.peers.send(
            self.buf.at[pl.ds(other, half)], self.landed, self.sends.at[p], self.recvs.at[p], bit
        )

    def finish(self, p):
        half = self.peers.count >> (p + 1)
        self.copy.wait()
        kept = pl.ds(self.offs[p + 1], half)
        self.buf[kept] += self.landed[...]


class Doubling:
    def __init__(self, halving, full, sends, recvs):
        self.halving, self.full, self.sends, self.recvs = halving, full, sends, recvs
        self.peers = halving.peers

    def load(self):
        place = pl.ds(self.halving.place, 1)
        self.full[place] = self.halving.buf[place]

    def start(self, p):
        half = self.peers.count >> (p + 1)
        owned = self.full.at[pl.ds(self.halving.offs[p + 1], half)]
        self.copy = self.peers.send(
            owned, owned, self.sends.at[p], self.recvs.at[p], self.halving.order[p]
        )

    def finish(self, p):
        self.copy.wait()


class SmallSum:
    def __init__(self, peers, order, sent, recv, sends, recvs):
        self.peers, self.order = peers, order
        self.sent, self.recv, self.sends, self.recvs = sent, recv, sends, recvs

    def start(self, p):
        self.copy = self.peers.send(
            self.sent.at[p], self.recv.at[p], self.sends.at[p], self.recvs.at[p], self.order[p]
        )

    def finish(self, p):
        self.copy.wait()
        self.sent[p + 1] = self.sent[p] + self.recv[p]


def fill_blocks(halvings, side, rows_ref, grads_ref):
    count = halvings[0].peers.count
    block = halvings[0].buf.shape[1]
    rows = rows_ref.shape[1]
    step = min(rows, max(block, 256))
    for first in range(0, rows, step):
        part = jnp.dot(
            rows_ref[side, pl.ds(first, step), :], grads_ref[...], preferred_element_type=jnp.float32
        )
        for b in range(step // block):
            rest = first // block + b
            for s, h in enumerate(halvings):
                spot = sum(
                    ((rest >> (bit - 1)) & 1) * (count >> (p + 1))
                    for p, bit in enumerate(h.order)
                    if p > 0
                )
                h.buf[side * (count // 2) + spot] = part[
                    b * block : (b + 1) * block, s * LANES : (s + 1) * LANES
                ]


def comm_kernel(count, state_streams, grad_streams, *refs):
    refs = list(refs)
    take = lambda k: [refs.pop(0) for _ in range(k)]
    has_state, has_grad = state_streams > 0, grad_streams > 0
    if has_state:
        state_ref, normal_ref = take(2)
    if has_grad:
        rows_ref, grads_ref = take(2)
    if has_state:
        state_out, normal_out = take(2)
    if has_grad:
        (grad_out,) = take(1)
    if has_state:
        state_bufs, state_recvs, state_full = (take(state_streams) for _ in range(3))
        small_sent, small_recv, small_s, small_r = take(4)
    if has_grad:
        grad_bufs, grad_recvs = (take(grad_streams) for _ in range(2))
    sends, recvs = take(2)

    peers = Peers(count)
    orders = phase_orders(count)
    depth = peers.depth
    sums, small, outs, grads = [], [], [], []
    slot = 0
    if has_state:
        for s in range(state_streams):
            sums.append(
                Halving(peers, orders[s % 3], state_bufs[s], state_recvs[s], sends.at[slot], recvs.at[slot])
            )
            outs.append(Doubling(sums[-1], state_full[s], sends.at[slot + 1], recvs.at[slot + 1]))
            slot += 2
            state_bufs[s][...] = state_ref[:, :, s * LANES : (s + 1) * LANES]
        small.append(SmallSum(peers, orders[0], small_sent, small_recv, small_s, small_r))
        small_sent[0] = normal_ref[...]
    if has_grad:
        for s in range(grad_streams):
            order = orders[(s + state_streams) % 3]
            grads.append(Halving(peers, order, grad_bufs[s], grad_recvs[s], sends.at[slot], recvs.at[slot]))
            slot += 1

    peers.greet()
    for h in sums + small:
        h.start(0)
    if has_grad:
        core = peers.bits[0]
        fill_blocks(grads, 1 - core, rows_ref, grads_ref)
        for h in grads:
            h.start(0)
        fill_blocks(grads, core, rows_ref, grads_ref)

    grad_steps = [(h, p) for p in range(depth) for h in grads]
    for p in range(depth):
        for h in sums + small:
            h.finish(p)
            if p + 1 < depth:
                h.start(p + 1)
            elif h in sums:
                gather = outs[sums.index(h)]
                gather.load()
                gather.start(depth - 1)
        if p % 2 == 1 or not has_state:
            for h in grads:
                step = p // 2 if has_state else p
                h.finish(step)
                if step + 1 < depth:
                    h.start(step + 1)
    done = depth // 2 if has_state else depth
    for p in reversed(range(depth)):
        for h in outs:
            h.finish(p)
            if p > 0:
                h.start(p - 1)
        if p % 2 == 0 and done < depth:
            for h in grads:
                h.finish(done)
                if done + 1 < depth:
                    h.start(done + 1)
            done += 1
    while done < depth:
        for h in grads:
            h.finish(done)
            if done + 1 < depth:
                h.start(done + 1)
        done += 1
    if has_state:
        for s in range(state_streams):
            state_out[:, :, s * LANES : (s + 1) * LANES] = state_full[s][...]
        normal_out[...] = small_sent[depth]
    for s, h in enumerate(grads):
        grad_out[:, s * LANES : (s + 1) * LANES] = h.buf[h.place]


def communicate(count, call, state=None, grad=None):
    depth = count.bit_length() - 1
    args, shapes, scratch = [], [], []
    f32 = jnp.float32
    state_streams = grad_streams = 0
    if state is not None:
        total, normal = state
        groups, head_dim, feats = total.shape
        rows = groups * head_dim // count
        args += [total.reshape(count, rows, feats), normal]
        shapes += [
            jax.ShapeDtypeStruct((count, rows, feats), f32),
            jax.ShapeDtypeStruct(normal.shape, f32),
        ]
        state_streams = feats // LANES
        scratch += [pltpu.VMEM((count, rows, LANES), f32)] * state_streams
        scratch += [pltpu.VMEM((count - 1, rows, LANES), f32)] * state_streams
        scratch += [pltpu.VMEM((count, rows, LANES), f32)] * state_streams
        scratch += [
            pltpu.VMEM((depth + 1,) + normal.shape, f32),
            pltpu.VMEM((depth,) + normal.shape, f32),
            pltpu.SemaphoreType.DMA((depth,)),
            pltpu.SemaphoreType.DMA((depth,)),
        ]
    if grad is not None:
        rows_t, grads = grad
        block = 2 * rows_t.shape[1] // count
        cols = grads.shape[1]
        args += [rows_t, grads]
        shapes.append(jax.ShapeDtypeStruct((block, cols), f32))
        grad_streams = cols // LANES
        scratch += [pltpu.VMEM((count, block, LANES), f32)] * grad_streams
        scratch += [pltpu.VMEM((count - 1, block, LANES), f32)] * grad_streams
    slots = 2 * state_streams + grad_streams
    scratch += [pltpu.SemaphoreType.DMA((slots, depth))] * 2
    out = pl.pallas_call(
        functools.partial(comm_kernel, count, state_streams, grad_streams),
        out_shape=tuple(shapes),
        in_specs=[pl.BlockSpec(memory_space=pltpu.VMEM)] * len(args),
        out_specs=tuple([pl.BlockSpec(memory_space=pltpu.VMEM)] * len(shapes)),
        scratch_shapes=scratch,
        compiler_params=pltpu.CompilerParams(
            collective_id=call, has_side_effects=True, vmem_limit_bytes=48 * 2**20
        ),
        name=f"exchange{call}",
    )(*args)
    out = list(out)
    if state is not None:
        out[0] = out[0].reshape(total.shape)
    return out


def features(rows, table, feat_count):
    logits = jnp.einsum("tgd,gdm->gtm", rows, table, precision=HIGHEST)
    half_norm = 0.5 * jnp.sum(rows * rows, axis=2).T
    return jnp.exp(logits - half_norm[:, :, None]) * feat_count ** (-0.5)


def feature_grad(rows, feats, grads, table, feature_scale, tok_count):
    weighted = feats * grads
    back = jnp.einsum("gtm,gdm->tgd", weighted, table, precision=HIGH)
    totals = jnp.sum(weighted, axis=2).T
    result = (back - rows * totals[:, :, None]) * feature_scale
    return result.reshape(tok_count, -1).astype(jnp.bfloat16)


def back_product(grads, weight):
    return lax.dot_general(
        grads, weight, (((1,), (1,)), ((), ())), preferred_element_type=jnp.float32
    )


def shards(count, hidden, query_weight, key_weight, values, grad_out, random_feats):
    tok_count, width = hidden.shape
    group_count, head_dim, feat_count = random_feats.shape
    feature_scale = head_dim ** (-0.25)
    rows_t = hidden.T.reshape(count // 2, 2, width // count, tok_count)
    rows_t = rows_t.transpose(1, 0, 2, 3).reshape(2, width // 2, tok_count)
    query_proj = jnp.dot(hidden, query_weight, preferred_element_type=jnp.float32)
    key_proj = jnp.dot(hidden, key_weight, preferred_element_type=jnp.float32)
    query_rows = (query_proj * feature_scale).reshape(tok_count, group_count, head_dim)
    key_rows = (key_proj * feature_scale).reshape(tok_count, group_count, head_dim)
    value_rows = values.astype(jnp.float32).reshape(tok_count, group_count, head_dim)
    key_feats = features(key_rows, random_feats, feat_count)
    local_state = jnp.einsum("tgj,gtm->gjm", value_rows, key_feats, precision=HIGH)
    local_normal = jnp.sum(key_feats, axis=1)
    value_state, normalizer = communicate(count, 0, state=(local_state, local_normal))
    query_feats = features(query_rows, random_feats, feat_count)
    numerator = jnp.einsum("gtm,gjm->tgj", query_feats, value_state, precision=HIGH)
    denominator = jnp.sum(query_feats * normalizer[:, None, :], axis=2).T
    attended = numerator / denominator[:, :, None]
    upstream = grad_out.astype(jnp.float32).reshape(tok_count, group_count, head_dim)
    grad_numer = upstream / denominator[:, :, None]
    grad_denom = -jnp.sum(upstream * attended, axis=2) / denominator
    grad_qfeat = (
        jnp.einsum("tgj,gjm->gtm", grad_numer, value_state, precision=HIGH)
        + grad_denom.T[:, :, None] * normalizer[:, None, :]
    )
    part_state = jnp.einsum("gtm,tgj->gjm", query_feats, grad_numer, precision=HIGH)
    part_normal = jnp.sum(query_feats * grad_denom.T[:, :, None], axis=1)
    grad_query = feature_grad(
        query_rows, query_feats, grad_qfeat, random_feats, feature_scale, tok_count
    )
    grad_state, grad_normal, grad_query_weight = communicate(
        count, 1, state=(part_state, part_normal), grad=(rows_t, grad_query)
    )
    grad_kfeat = (
        jnp.einsum("tgj,gjm->gtm", value_rows, grad_state, precision=HIGH) + grad_normal[:, None, :]
    )
    grad_value = jnp.einsum("gtm,gjm->tgj", key_feats, grad_state, precision=HIGH)
    grad_values = grad_value.reshape(tok_count, -1).astype(jnp.bfloat16)
    grad_key = feature_grad(key_rows, key_feats, grad_kfeat, random_feats, feature_scale, tok_count)
    (grad_key_weight,) = communicate(count, 2, grad=(rows_t, grad_key))
    both_parts = back_product(grad_query, query_weight) + back_product(grad_key, key_weight)
    grad_hidden = both_parts
    return (grad_hidden, grad_values, grad_query_weight, grad_key_weight)


def solution(mesh):
    placed = (
        P("seq", None),
        P(None, "head"),
        P(None, "head"),
        P("seq", "head"),
        P("seq", "head"),
        P("head", None, None),
    )

    def local(*args):
        out = shards(mesh.shape["seq"], *args)
        if mesh.shape["head"] == 1:
            return out
        return (lax.psum(out[0], "head"),) + tuple(out[1:])

    return jax.shard_map(
        local,
        mesh=mesh,
        in_specs=placed,
        out_specs=(P("seq", None), P("seq", "head"), P("seq", "head"), P("seq", "head")),
        check_vma=False,
    )
```

time: 407 us -> 113 us (0.28)
  waiting for transfers between devices: 269 us -> 0 us
  Pallas kernels: 0 us -> 85.7 us
  blocking collectives: 81.4 us -> 0 us
  matrix products: 30.9 us -> 14 us
  between operations: 14.2 us -> 0.91 us
    unnamed x3 -> x0, waiting for transfers between devices: 138 us -> none
    psum x1 -> x0, waiting for transfers between devices: 131 us -> none  [shards(): value_state, normalizer = lax.psum((local_state, local_normal), 'seq')]
    pallas_call x0 -> x3, Pallas kernels: none -> 85.7 us  [communicate(): pl.pallas_call(functools.partial(comm_kernel, count, state_streams, grad_...]
    psum x2 -> x0, blocking collectives: 81.4 us -> none  [the longest x1 42.1 us: shards(): value_state, normalizer = lax.psum((local_state, local_normal), 'seq')]
    dot_general x5 -> x2, matrix products: 7.74 us -> 3.4 us  [features(): logits = jnp.einsum('tgd,gdm->gtm', rows, table, precision=HIGHEST)]
  transfers between devices with their start and end apart: 2 -> 0, of which waited for: 2 -> 0; matrix products, arithmetic and copies ran while one was open for 1% -> 0% of each run, Pallas kernels for 0% -> 0%
where the time goes in v1:
time: 113 us; the launch traced here: 112 us
  Pallas kernels  85.7 us (76%)
  matrix products  14 us (12%)
  local copies, waits for them, and re-layouts  10.8 us (10%)
    pallas_call x3, Pallas kernels, communicate(): pl.pallas_call(functools.partial(comm_kernel, count, state_streams, grad_...  85.7 us
    unnamed x35, local copies, waits for them, and re-layouts  6.79 us
    dot_general x2, matrix products, features(): logits = jnp.einsum('tgd,gdm->gtm', rows, table, precision=HIGHEST)  3.4 us
    dot_general x2, matrix products, back_product(): lax.dot_general(grads, weight, (((1,), (1,)), ((), ())), preferred_elemen...  2.54 us

profile of v1, /device:TPU:0, one launch (start us, length us, event | category | flops | bytes accessed | tf_op | source)
XLA Modules:
  0.0 112.3 jit_solution(5445334944183782520)
XLA Ops:
  0.6 1.7 %convolution_multiply_fusion = f32[128,512]{1,0:T(8,128)S(1)} fusion(bf16[128,1024]{1,0:T(8,128)(2,1)} %param.6, bf16[1024,512]{1,0:T(8,128)(2,1)} %param.8), kind=kOutput, calls=%fused_computation.20 | convolution fusion | flops 134283264 | bytes 1572864 | tf_op jit(solution)/shard_map/dot_general | solution.py:303
  2.5 0.9 copy-done.3
  3.4 1.2 %fusion.22 = (f32[8,256]{1,0:T(8,128)S(1)}, f32[8,128,256]{2,1,0:T(8,128)S(1)}) fusion(f32[8,128]{1,0:T(8,128)S(1)} %multiply_bitcast_fusion, f32[128,8,64]{0,2,1:T(8,128)S(1)} %bitcast.93, f32[8,64,256]{2,1,0:T(8,128)S(1)} %copy-done.3), kind=kOutput, calls=%fused_computation.43 | convolution fusion | flops 202110976 | bytes 1847296 | tf_op jit(solution)/shard_map/tgd,gdm->gtm/dot_general | solution.py:277
  5.6 32.3 %exchange0.1 = (f32[32,16,256]{2,1,0:T(8,128)S(1)}, f32[8,256]{1,0:T(8,128)S(1)}) custom-call(f32[32,16,256]{2,1,0:T(8,128)S(1)} %bitcast.90, f32[8,256]{1,0:T(8,128)S(1)} %get-tuple-element.24.refs_1_), custom_call_target="tpu_custom_call" | custom-call | tf_op jit(solution)/shard_map/exchange0/pallas_call | solution.py:259
  37.9 0.6 broadcast_multiply_fusion
  39.0 0.6 copy-done.5
  39.7 2.2 %multiply_reduce_fusion.1 = (f32[8,128]{1,0:T(8,128)S(1)}, f32[8,128,256]{2,1,0:T(8,128)S(1)}) fusion(f32[8,256]{1,0:T(8,128)S(1)} %copy-done.14, f32[8,128]{1,0:T(8,128)S(1)} %multiply_bitcast_fusion.1, f32[128,8,64]{0,2,1:T(8,128)} %bitcast.95, f32[8,64,256]{2,1,0:T(8,128)S(1)} %copy-done.3), kind=kOutput, calls=%fused_computation.27 | convolution fusion | flops 202112000 | bytes 1851392 | tf_op jit(solution)/shard_map/tgd,gdm->gtm/dot_general | solution.py:277
  41.9 1.7 %copy.23 = f32[128,512]{0,1:T(8,128)} copy(bf16[128,512]{1,0:T(8,128)(2,1)} %param.10) | data formatting | bytes 393216 | tf_op jit(solution)/shard_map/reshape | solution.py:315
  43.7 1.7 %fusion.14 = f32[128,8]{0,1:T(8,128)S(1)} fusion(f32[128,8,64]{0,2,1:T(8,128)} %bitcast.97, f32[8,64,256]{2,1,0:T(8,128)S(1)} %bitcast.88, f32[8,128,256]{2,1,0:T(8,128)S(1)} %get-tuple-element.27, f32[128,8]{0,1:T(8,128)S(1)} %bitcast.108), kind=kOutput, calls=%fused_computation.25 | convolution fusion | flops 101121024 | bytes 1843200 | tf_op jit(solution)/shard_map/gtm,gjm->tgj/dot_general | solution.py:312
  45.4 0.9 fusion.23
  46.4 0.7 fusion.12
  47.1 1.3 %fusion.26 = f32[128,1024]{1,0:T(8,128)} fusion(bf16[128,512]{0,1:T(8,128)(2,1)S(1)} %bitcast.104, bf16[1024,512]{1,0:T(8,128)(2,1)S(1)} %copy-done), kind=kOutput, calls=%fused_computation.47 | convolution fusion | flops 134217728 | bytes 1703936 | tf_op jit(solution)/shard_map/dot_general | solution.py:291
  49.0 0.7 copy-done.10
  49.8 0.9 copy.26
  50.6 1.0 copy.27
  51.6 1.0 copy.28.refs_3_
  52.6 32.1 %exchange1.1 = (f32[32,16,256]{2,1,0:T(8,128)S(1)}, f32[8,256]{1,0:T(8,128)S(1)}, f32[32,512]{1,0:T(8,128)S(1)}) custom-call(f32[32,16,256]{2,1,0:T(8,128)S(1)} %bitcast.87, f32[8,256]{1,0:T(8,128)S(1)} %multiply_reduce_fusion.refs_1_, bf16[2,512,128]{2,1,0:T(8,128)(2,1)S(1)} %bitcast.85, bf16[128,512]{1,0:T(8,128)(2,1)S(1)} %copy.28.refs_3_), custom_call_target="tpu_custom_call" | custom-call | tf_op jit(solution)/shard_map/exchange1/pallas_call | solution.py:259
  85.8 0.7 fusion.13
  86.9 1.3 %convolution_add_fusion.2 = f32[128,1024]{1,0:T(8,128)} fusion(f32[128,1024]{1,0:T(8,128)S(1)} %copy-done.11, bf16[128,512]{0,1:T(8,128)(2,1)S(1)} %bitcast.100, bf16[1024,512]{1,0:T(8,128)(2,1)S(1)} %copy-done.7), kind=kOutput, calls=%fused_computation.10 | convolution fusion | flops 134348800 | bytes 2228224 | tf_op jit(solution)/shard_map/dot_general | solution.py:291
  88.2 0.7 convolution_convert_fusion
  88.8 0.8 copy.31
  89.7 21.3 %exchange2.1 = f32[32,512]{1,0:T(8,128)S(1)} custom-call(bf16[2,512,128]{2,1,0:T(8,128)(2,1)S(1)} %bitcast.86, bf16[128,512]{1,0:T(8,128)(2,1)S(1)} %copy.30.refs_1_), custom_call_target="tpu_custom_call" | custom-call | tf_op jit(solution)/shard_map/exchange2/pallas_call | solution.py:259
  111.1 0.6 copy.35
  111.7 0.6 copy.36
  (41 shorter events, 4.0 us)
Async XLA Ops:
  0.6 37.9 %copy-start = (bf16[1024,512]{1,0:T(8,128)(2,1)S(1)}, bf16[1024,512]{1,0:T(8,128)(2,1)}, u32[]{:S(2)}) copy-start(bf16[1024,512]{1,0:T(8,128)(2,1)} %param.7) | copy-start | bytes 3145732
  2.4 1.0 copy-start.3
  3.4 1.2 %copy-start.13 = (bf16[128,512]{1,0:T(8,128)(2,1)S(1)}, bf16[128,512]{1,0:T(8,128)(2,1)}, u32[]{:S(2)}) copy-start(bf16[128,512]{1,0:T(8,128)(2,1)} %param.9) | copy-start | bytes 393220
  4.6 1.0 copy-start.1
  5.6 32.9 %copy-start.9 = (bf16[128,1024]{1,0:T(8,128)(2,1)S(1)}, bf16[128,1024]{1,0:T(8,128)(2,1)}, u32[]{:S(2)}) copy-start(bf16[128,1024]{1,0:T(8,128)(2,1)} %param.6) | copy-start | bytes 786436
  38.9 0.7 copy-start.5
  39.0 0.7 copy-start.14
  43.7 1.7 %copy-start.8 = (f32[128,512]{0,1:T(8,128)S(1)}, f32[128,512]{0,1:T(8,128)}, u32[]{:S(2)}) copy-start(f32[128,512]{0,1:T(8,128)} %copy.23) | copy-start | bytes 786436
  45.4 1.0 copy-start.6
  47.0 1.3 %copy-start.12 = (bf16[128,8,64]{0,2,1:T(8,128)(2,1)}, bf16[128,8,64]{0,2,1:T(8,128)(2,1)S(1)}, u32[]{:S(2)}) copy-start(bf16[128,8,64]{0,2,1:T(8,128)(2,1)S(1)} %fusion.12) | copy-start | bytes 393220
  48.8 1.0 copy-start.10
  49.8 34.9 %copy-start.2 = (f32[8,128,256]{2,1,0:T(8,128)S(1)}, f32[8,128,256]{2,1,0:T(8,128)}, u32[]{:S(2)}) copy-start(f32[8,128,256]{2,1,0:T(8,128)} %copy-done.1) | copy-start | bytes 3145732
  84.7 1.0 copy-start.4
  85.3 1.3 %copy-start.7 = (bf16[1024,512]{1,0:T(8,128)(2,1)S(1)}, bf16[1024,512]{1,0:T(8,128)(2,1)}, u32[]{:S(2)}) copy-start(bf16[1024,512]{1,0:T(8,128)(2,1)} %param.8) | copy-start | bytes 3145732
  85.8 1.1 copy-start.11

commit v2 on v1

--- a/solution.py
+++ b/solution.py
@@ -15,7 +15,15 @@
 def phase_orders(count):
     depth = count.bit_length() - 1
     middle = list(range(1, depth - 1))
-    return [[0] + middle[s:] + middle[:s] + [depth - 1] for s in range(3)]
+    return [
+        [(bit,) for bit in [0] + middle[s:] + middle[:s] + [depth - 1]] for s in range(3)
+    ]
+
+
+def wide_orders(count):
+    depth = count.bit_length() - 1
+    pairs = [tuple(range(b, min(b + 2, depth))) for b in range(1, depth, 2)]
+    return [[(0,)] + pairs, [(0,)] + pairs[::-1]]
 
 
 class Peers:
@@ -24,72 +32,104 @@
         self.depth = count.bit_length() - 1
         self.me = lax.axis_index("seq")
         self.bits = [(self.me // 2**b) % 2 for b in range(self.depth)]
-        self.ids = [self.me + (1 - 2 * self.bits[b]) * 2**b for b in range(self.depth)]
-
-    def greet(self):
+
+    def reach(self, group):
+        found = []
+        for mask in range(1, 2 ** len(group)):
+            index, digit, flips = self.me, 0, 0
+            for j, b in enumerate(group):
+                bit = self.bits[b]
+                if (mask >> j) & 1:
+                    index = index + (1 - 2 * bit) * 2**b
+                    bit = 1 - bit
+                    flips += 2**b
+                digit = 2 * digit + bit
+            found.append((flips, index, digit))
+        return found
+
+    def greet(self, orders):
+        met = {}
+        for order in orders:
+            for group in order:
+                for flips, index, _ in self.reach(group):
+                    met[flips] = index
         barrier = pltpu.get_barrier_semaphore()
-        for peer in self.ids:
+        for flips in sorted(met):
             pl.semaphore_signal(
-                barrier, inc=1, device_id={"seq": peer}, device_id_type=pl.DeviceIdType.MESH
+                barrier, inc=1, device_id={"seq": met[flips]}, device_id_type=pl.DeviceIdType.MESH
             )
-        pl.semaphore_wait(barrier, self.depth)
-
-    def send(self, src, dst, sends, recvs, bit):
-        copy = pltpu.make_async_remote_copy(
-            src_ref=src,
-            dst_ref=dst,
-            send_sem=sends,
-            recv_sem=recvs,
-            device_id={"seq": self.ids[bit]},
-            device_id_type=pl.DeviceIdType.MESH,
-        )
-        copy.start()
-        return copy
+        pl.semaphore_wait(barrier, len(met))
+
+
+def send(src, dst, sends, recvs, index):
+    copy = pltpu.make_async_remote_copy(
+        src_ref=src,
+        dst_ref=dst,
+        send_sem=sends,
+        recv_sem=recvs,
+        device_id={"seq": index},
+        device_id_type=pl.DeviceIdType.MESH,
+    )
+    copy.start()
+    return copy
 
 
 class Halving:
     def __init__(self, peers, order, buf, recv, sends, recvs):
         self.peers, self.order = peers, order
         self.buf, self.recv, self.sends, self.recvs = buf, recv, sends, recvs
-        self.offs = [0]
-        for p, bit in enumerate(order):
-            self.offs.append(self.offs[-1] + peers.bits[bit] * (peers.count >> (p + 1)))
+        self.offs, self.sizes = [0], [peers.count]
+        for group in order:
+            size = self.sizes[-1] // 2 ** len(group)
+            digit = 0
+            for b in group:
+                digit = 2 * digit + peers.bits[b]
+            self.offs.append(self.offs[-1] + digit * size)
+            self.sizes.append(size)
         self.place = self.offs[-1]
+        self.steps = len(order)
 
     def start(self, p):
-        half = self.peers.count >> (p + 1)
-        bit = self.order[p]
-        other = self.offs[p] + (1 - self.peers.bits[bit]) * half
-        self.landed = self.recv.at[pl.ds(self.peers.count - 2 * half, half)]
-        self.copy = self.peers.send(
-            self.buf.at[pl.ds(other, half)], self.landed, self.sends.at[p], self.recvs.at[p], bit
-        )
+        size = self.sizes[p + 1]
+        base = self.peers.count - self.sizes[p]
+        self.copies, self.landed = [], []
+        for m, (_, index, digit) in enumerate(self.peers.reach(self.order[p])):
+            slot = self.recv.at[pl.ds(base + m * size, size)]
+            self.landed.append(slot)
+            part = self.buf.at[pl.ds(self.offs[p] + digit * size, size)]
+            self.copies.append(
+                send(part, slot, self.sends.at[3 * p + m], self.recvs.at[3 * p + m], index)
+            )
 
     def finish(self, p):
-        half = self.peers.count >> (p + 1)
-        self.copy.wait()
-        kept = pl.ds(self.offs[p + 1], half)
-        self.buf[kept] += self.landed[...]
+        kept = pl.ds(self.offs[p + 1], self.sizes[p + 1])
+        for copy in self.copies:
+            copy.wait()
+        total = self.landed[0][...]
+        for slot in self.landed[1:]:
+            total = total + slot[...]
+        self.buf[kept] += total
 
 
 class Doubling:
     def __init__(self, halving, full, sends, recvs):
         self.halving, self.full, self.sends, self.recvs = halving, full, sends, recvs
-        self.peers = halving.peers
 
     def load(self):
         place = pl.ds(self.halving.place, 1)
         self.full[place] = self.halving.buf[place]
 
     def start(self, p):
-        half = self.peers.count >> (p + 1)
-        owned = self.full.at[pl.ds(self.halving.offs[p + 1], half)]
-        self.copy = self.peers.send(
-            owned, owned, self.sends.at[p], self.recvs.at[p], self.halving.order[p]
-        )
+        h = self.halving
+        owned = self.full.at[pl.ds(h.offs[p + 1], h.sizes[p + 1])]
+        self.copies = [
+            send(owned, owned, self.sends.at[3 * p + m], self.recvs.at[3 * p + m], index)
+            for m, (_, index, _) in enumerate(h.peers.reach(h.order[p]))
+        ]
 
     def finish(self, p):
-        self.copy.wait()
+        for copy in self.copies:
+            copy.wait()
 
 
 class SmallSum:
@@ -98,13 +138,24 @@
         self.sent, self.recv, self.sends, self.recvs = sent, recv, sends, recvs
 
     def start(self, p):
-        self.copy = self.peers.send(
-            self.sent.at[p], self.recv.at[p], self.sends.at[p], self.recvs.at[p], self.order[p]
-        )
+        self.copies = [
+            send(
+                self.sent.at[p],
+                self.recv.at[3 * p + m],
+                self.sends.at[3 * p + m],
+                self.recvs.at[3 * p + m],
+                index,
+            )
+            for m, (_, index, _) in enumerate(self.peers.reach(self.order[p]))
+        ]
 
     def finish(self, p):
-        self.copy.wait()
-        self.sent[p + 1] = self.sent[p] + self.recv[p]
+        for copy in self.copies:
+            copy.wait()
+        total = self.sent[p]
+        for m in range(len(self.copies)):
+            total = total + self.recv[3 * p + m]
+        self.sent[p + 1] = total
 
 
 def fill_blocks(halvings, side, rows_ref, grads_ref):
@@ -121,7 +172,7 @@
             for s, h in enumerate(halvings):
                 spot = sum(
                     ((rest >> (bit - 1)) & 1) * (count >> (p + 1))
-                    for p, bit in enumerate(h.order)
+                    for p, bit in enumerate(sum(h.order, ()))
                     if p > 0
                 )
                 h.buf[side * (count // 2) + spot] = part[
@@ -149,19 +200,19 @@
     sends, recvs = take(2)
 
     peers = Peers(count)
-    orders = phase_orders(count)
-    depth = peers.depth
+    orders, wide = phase_orders(count), wide_orders(count)
+    depth, steps = peers.depth, len(wide[0])
     sums, small, outs, grads = [], [], [], []
     slot = 0
     if has_state:
         for s in range(state_streams):
             sums.append(
-                Halving(peers, orders[s % 3], state_bufs[s], state_recvs[s], sends.at[slot], recvs.at[slot])
+                Halving(peers, wide[s % 2], state_bufs[s], state_recvs[s], sends.at[slot], recvs.at[slot])
             )
             outs.append(Doubling(sums[-1], state_full[s], sends.at[slot + 1], recvs.at[slot + 1]))
             slot += 2
             state_bufs[s][...] = state_ref[:, :, s * LANES : (s + 1) * LANES]
-        small.append(SmallSum(peers, orders[0], small_sent, small_recv, small_s, small_r))
+        small.append(SmallSum(peers, wide[0], small_sent, small_recv, small_s, small_r))
         small_sent[0] = normal_ref[...]
     if has_grad:
         for s in range(grad_streams):
@@ -169,7 +220,7 @@
             grads.append(Halving(peers, order, grad_bufs[s], grad_recvs[s], sends.at[slot], recvs.at[slot]))
             slot += 1
 
-    peers.greet()
+    peers.greet([h.order for h in sums + grads])
     for h in sums + small:
         h.start(0)
     if has_grad:
@@ -179,44 +230,41 @@
             h.start(0)
         fill_blocks(grads, core, rows_ref, grads_ref)
 
-    grad_steps = [(h, p) for p in range(depth) for h in grads]
-    for p in range(depth):
-        for h in sums + small:
-            h.finish(p)
-            if p + 1 < depth:
-                h.start(p + 1)
-            elif h in sums:
-                gather = outs[sums.index(h)]
-                gather.load()
-                gather.start(depth - 1)
-        if p % 2 == 1 or not has_state:
-            for h in grads:
-                step = p // 2 if has_state else p
+    def advance(step):
+        for h in grads:
+            if step < depth:
                 h.finish(step)
-                if step + 1 < depth:
-                    h.start(step + 1)
-    done = depth // 2 if has_state else depth
-    for p in reversed(range(depth)):
-        for h in outs:
-            h.finish(p)
+            if step + 1 < depth:
+                h.start(step + 1)
+
+    done = 0
+    if has_state:
+        for p in range(steps):
+            for h in sums + small:
+                h.finish(p)
+                if p + 1 < steps:
+                    h.start(p + 1)
+                elif h in sums:
+                    gather = outs[sums.index(h)]
+                    gather.load()
+                    gather.start(steps - 1)
             if p > 0:
-                h.start(p - 1)
-        if p % 2 == 0 and done < depth:
-            for h in grads:
-                h.finish(done)
-                if done + 1 < depth:
-                    h.start(done + 1)
-            done += 1
-    while done < depth:
-        for h in grads:
-            h.finish(done)
-            if done + 1 < depth:
-                h.start(done + 1)
-        done += 1
+                advance(done)
+                done += 1
+        for p in reversed(range(steps)):
+            for h in outs:
+                h.finish(p)
+                if p > 0:
+                    h.start(p - 1)
+            if p > 0:
+                advance(done)
+                done += 1
+    for step in range(done, depth):
+        advance(step)
     if has_state:
         for s in range(state_streams):
             state_out[:, :, s * LANES : (s + 1) * LANES] = state_full[s][...]
-        normal_out[...] = small_sent[depth]
+        normal_out[...] = small_sent[steps]
     for s, h in enumerate(grads):
         grad_out[:, s * LANES : (s + 1) * LANES] = h.buf[h.place]
 
@@ -241,9 +289,9 @@
         scratch += [pltpu.VMEM((count, rows, LANES), f32)] * state_streams
         scratch += [
             pltpu.VMEM((depth + 1,) + normal.shape, f32),
-            pltpu.VMEM((depth,) + normal.shape, f32),
-            pltpu.SemaphoreType.DMA((depth,)),
-            pltpu.SemaphoreType.DMA((depth,)),
+            pltpu.VMEM((3 * depth,) + normal.shape, f32),
+            pltpu.SemaphoreType.DMA((3 * depth,)),
+            pltpu.SemaphoreType.DMA((3 * depth,)),
         ]
     if grad is not None:
         rows_t, grads = grad
@@ -255,7 +303,7 @@
         scratch += [pltpu.VMEM((count, block, LANES), f32)] * grad_streams
         scratch += [pltpu.VMEM((count - 1, block, LANES), f32)] * grad_streams
     slots = 2 * state_streams + grad_streams
-    scratch += [pltpu.SemaphoreType.DMA((slots, depth))] * 2
+    scratch += [pltpu.SemaphoreType.DMA((slots, 3 * depth))] * 2
     out = pl.pallas_call(
         functools.partial(comm_kernel, count, state_streams, grad_streams),
         out_shape=tuple(shapes),

time: 113 us -> 104 us (0.920)
  Pallas kernels: 85.7 us -> 76.5 us
    pallas_call x3, Pallas kernels: 85.7 us -> 76.5 us  [communicate(): pl.pallas_call(functools.partial(comm_kernel, count, state_streams, grad_...]
where the time goes in v2:
time: 104 us; the launch traced here: 103 us
  Pallas kernels  76.5 us (74%)
  matrix products  14 us (13%)
  local copies, waits for them, and re-layouts  10.8 us (10%)
    pallas_call x3, Pallas kernels, communicate(): pl.pallas_call(functools.partial(comm_kernel, count, state_streams, grad_...  76.5 us
    unnamed x35, local copies, waits for them, and re-layouts  6.78 us
    dot_general x2, matrix products, features(): logits = jnp.einsum('tgd,gdm->gtm', rows, table, precision=HIGHEST)  3.4 us
    dot_general x2, matrix products, back_product(): lax.dot_general(grads, weight, (((1,), (1,)), ((), ())), preferred_elemen...  2.54 us

profile of v2, /device:TPU:0, one launch (start us, length us, event | category | flops | bytes accessed | tf_op | source)
XLA Modules:
  0.0 103.2 jit_solution(16273467487302675319)
XLA Ops:
  0.6 1.7 %convolution_multiply_fusion = f32[128,512]{1,0:T(8,128)S(1)} fusion(bf16[128,1024]{1,0:T(8,128)(2,1)} %param.6, bf16[1024,512]{1,0:T(8,128)(2,1)} %param.8), kind=kOutput, calls=%fused_computation.20 | convolution fusion | flops 134283264 | bytes 1572864 | tf_op jit(solution)/shard_map/dot_general | solution.py:351
  2.5 0.9 copy-done.3
  3.4 1.2 %fusion.22 = (f32[8,256]{1,0:T(8,128)S(1)}, f32[8,128,256]{2,1,0:T(8,128)S(1)}) fusion(f32[8,128]{1,0:T(8,128)S(1)} %multiply_bitcast_fusion, f32[128,8,64]{0,2,1:T(8,128)S(1)} %bitcast.93, f32[8,64,256]{2,1,0:T(8,128)S(1)} %copy-done.3), kind=kOutput, calls=%fused_computation.43 | convolution fusion | flops 202110976 | bytes 1847296 | tf_op jit(solution)/shard_map/tgd,gdm->gtm/dot_general | solution.py:325
  5.6 25.0 %exchange0.1 = (f32[32,16,256]{2,1,0:T(8,128)S(1)}, f32[8,256]{1,0:T(8,128)S(1)}) custom-call(f32[32,16,256]{2,1,0:T(8,128)S(1)} %bitcast.90, f32[8,256]{1,0:T(8,128)S(1)} %get-tuple-element.24.refs_1_), custom_call_target="tpu_custom_call" | custom-call | tf_op jit(solution)/shard_map/exchange0/pallas_call | solution.py:307
  31.7 0.6 copy-done.5
  32.4 2.2 %multiply_reduce_fusion.1 = (f32[8,128]{1,0:T(8,128)S(1)}, f32[8,128,256]{2,1,0:T(8,128)S(1)}) fusion(f32[8,256]{1,0:T(8,128)S(1)} %copy-done.14, f32[8,128]{1,0:T(8,128)S(1)} %multiply_bitcast_fusion.1, f32[128,8,64]{0,2,1:T(8,128)} %bitcast.95, f32[8,64,256]{2,1,0:T(8,128)S(1)} %copy-done.3), kind=kOutput, calls=%fused_computation.27 | convolution fusion | flops 202112000 | bytes 1851392 | tf_op jit(solution)/shard_map/tgd,gdm->gtm/dot_general | solution.py:325
  34.6 1.7 %copy.23 = f32[128,512]{0,1:T(8,128)} copy(bf16[128,512]{1,0:T(8,128)(2,1)} %param.10) | data formatting | bytes 393216 | tf_op jit(solution)/shard_map/reshape | solution.py:363
  36.4 1.7 %fusion.14 = f32[128,8]{0,1:T(8,128)S(1)} fusion(f32[128,8,64]{0,2,1:T(8,128)} %bitcast.97, f32[8,64,256]{2,1,0:T(8,128)S(1)} %bitcast.88, f32[8,128,256]{2,1,0:T(8,128)S(1)} %get-tuple-element.27, f32[128,8]{0,1:T(8,128)S(1)} %bitcast.108), kind=kOutput, calls=%fused_computation.25 | convolution fusion | flops 101121024 | bytes 1843200 | tf_op jit(solution)/shard_map/gtm,gjm->tgj/dot_general | solution.py:360
  38.1 0.9 fusion.23
  39.1 0.7 fusion.12
  39.7 1.3 %fusion.26 = f32[128,1024]{1,0:T(8,128)} fusion(bf16[128,512]{0,1:T(8,128)(2,1)S(1)} %bitcast.104, bf16[1024,512]{1,0:T(8,128)(2,1)S(1)} %copy-done), kind=kOutput, calls=%fused_computation.47 | convolution fusion | flops 134217728 | bytes 1703936 | tf_op jit(solution)/shard_map/dot_general | solution.py:339
  41.7 0.7 copy-done.10
  42.4 0.9 copy.26
  43.3 1.0 copy.27
  44.3 1.0 copy.28.refs_3_
  45.3 29.3 %exchange1.1 = (f32[32,16,256]{2,1,0:T(8,128)S(1)}, f32[8,256]{1,0:T(8,128)S(1)}, f32[32,512]{1,0:T(8,128)S(1)}) custom-call(f32[32,16,256]{2,1,0:T(8,128)S(1)} %bitcast.87, f32[8,256]{1,0:T(8,128)S(1)} %multiply_reduce_fusion.refs_1_, bf16[2,512,128]{2,1,0:T(8,128)(2,1)S(1)} %bitcast.85, bf16[128,512]{1,0:T(8,128)(2,1)S(1)} %copy.28.refs_3_), custom_call_target="tpu_custom_call" | custom-call | tf_op jit(solution)/shard_map/exchange1/pallas_call | solution.py:307
  74.6 0.6 fusion.24
  75.6 0.7 fusion.13
  76.7 1.3 %convolution_add_fusion.2 = f32[128,1024]{1,0:T(8,128)} fusion(f32[128,1024]{1,0:T(8,128)S(1)} %copy-done.11, bf16[128,512]{0,1:T(8,128)(2,1)S(1)} %bitcast.100, bf16[1024,512]{1,0:T(8,128)(2,1)S(1)} %copy-done.7), kind=kOutput, calls=%fused_computation.10 | convolution fusion | flops 134348800 | bytes 2228224 | tf_op jit(solution)/shard_map/dot_general | solution.py:339
  78.0 0.7 convolution_convert_fusion
  78.7 0.8 copy.31
  79.6 22.3 %exchange2.1 = f32[32,512]{1,0:T(8,128)S(1)} custom-call(bf16[2,512,128]{2,1,0:T(8,128)(2,1)S(1)} %bitcast.86, bf16[128,512]{1,0:T(8,128)(2,1)S(1)} %copy.30.refs_1_), custom_call_target="tpu_custom_call" | custom-call | tf_op jit(solution)/shard_map/exchange2/pallas_call | solution.py:307
  101.9 0.6 copy.35
  102.5 0.6 copy.36
  (41 shorter events, 4.0 us)
Async XLA Ops:
  0.6 30.5 %copy-start = (bf16[1024,512]{1,0:T(8,128)(2,1)S(1)}, bf16[1024,512]{1,0:T(8,128)(2,1)}, u32[]{:S(2)}) copy-start(bf16[1024,512]{1,0:T(8,128)(2,1)} %param.7) | copy-start | bytes 3145732
  2.4 1.0 %copy-start.3 = (f32[8,64,256]{2,1,0:T(8,128)S(1)}, f32[8,64,256]{2,1,0:T(8,128)}, u32[]{:S(2)}) copy-start(f32[8,64,256]{2,1,0:T(8,128)} %param.11) | copy-start | bytes 1572868
  3.4 1.2 %copy-start.13 = (bf16[128,512]{1,0:T(8,128)(2,1)S(1)}, bf16[128,512]{1,0:T(8,128)(2,1)}, u32[]{:S(2)}) copy-start(bf16[128,512]{1,0:T(8,128)(2,1)} %param.9) | copy-start | bytes 393220
  4.6 1.0 copy-start.1
  5.6 25.6 %copy-start.9 = (bf16[128,1024]{1,0:T(8,128)(2,1)S(1)}, bf16[128,1024]{1,0:T(8,128)(2,1)}, u32[]{:S(2)}) copy-start(bf16[128,1024]{1,0:T(8,128)(2,1)} %param.6) | copy-start | bytes 786436
  31.6 0.7 copy-start.5
  31.7 0.7 copy-start.14
  36.3 1.7 %copy-start.8 = (f32[128,512]{0,1:T(8,128)S(1)}, f32[128,512]{0,1:T(8,128)}, u32[]{:S(2)}) copy-start(f32[128,512]{0,1:T(8,128)} %copy.23) | copy-start | bytes 786436
  38.1 1.0 copy-start.6
  39.7 1.3 %copy-start.12 = (bf16[128,8,64]{0,2,1:T(8,128)(2,1)}, bf16[128,8,64]{0,2,1:T(8,128)(2,1)S(1)}, u32[]{:S(2)}) copy-start(bf16[128,8,64]{0,2,1:T(8,128)(2,1)S(1)} %fusion.12) | copy-start | bytes 393220
  41.5 1.0 copy-start.10
  42.4 32.1 %copy-start.2 = (f32[8,128,256]{2,1,0:T(8,128)S(1)}, f32[8,128,256]{2,1,0:T(8,128)}, u32[]{:S(2)}) copy-start(f32[8,128,256]{2,1,0:T(8,128)} %copy-done.1) | copy-start | bytes 3145732
  74.6 1.0 %copy-start.4 = (f32[8,64,256]{2,1,0:T(8,128)S(1)}, f32[8,64,256]{2,1,0:T(8,128)}, u32[]{:S(2)}) copy-start(f32[8,64,256]{2,1,0:T(8,128)} %param.11) | copy-start | bytes 1572868
  75.2 1.3 %copy-start.7 = (bf16[1024,512]{1,0:T(8,128)(2,1)S(1)}, bf16[1024,512]{1,0:T(8,128)(2,1)}, u32[]{:S(2)}) copy-start(bf16[1024,512]{1,0:T(8,128)(2,1)} %param.8) | copy-start | bytes 3145732
  75.6 1.1 %copy-start.11 = (f32[128,1024]{1,0:T(8,128)S(1)}, f32[128,1024]{1,0:T(8,128)}, u32[]{:S(2)}) copy-start(f32[128,1024]{1,0:T(8,128)} %fusion.26) | copy-start | bytes 1572868
